TPU v7x, 512 devices: a 8x2x16 block of a 8x16x16 slice. The times are simulated.
512 devices in a mesh: parts: 2 (over y), blk: 16 (over z), sub: 8 (over x), rep: 2 (over core).
Axes of the slice: x: 8, y: 2, z: 16, core: 2. Of those that a mesh axis runs over, the one named last changes fastest.
The devices are a block of a 8x16x16 slice.
Arguments:
- queries: bfloat16 [2048, 32, 128], P(('parts', 'blk', 'sub', 'rep')), parts along dimension 0, may hold values from -1.5 to 1.5
- passages: bfloat16 [2048, 128, 128], P(('parts', 'blk')), parts along dimension 0, may hold values from -1.5 to 1.5
- lengths: int32 [2048], P(('parts', 'blk')), parts along dimension 0, may hold values from 8 to 128
- slot_of: int32 [2048], P('parts'), parts along dimension 0, may hold values from 0 to 1023, each once
- candidates: int32 [2048, 256], P(('parts', 'blk', 'sub', 'rep')), parts along dimension 0, may hold values from 0 to 1023
Outputs:
- score: float32 [2048, 256], P(('parts', 'blk', 'sub', 'rep')), parts along dimension 0
- top: float32 [2048, 10], P(('parts', 'blk', 'sub', 'rep')), parts along dimension 0
There are 2 independent parts, one for each index of `parts`. A program takes and returns all parts, laid end to end along the dimension named above; each array names one. Nothing has to cross between parts.
Inputs may be any that keep to these rules, and one draw needn't show every extreme that they name: `slot_of`: a permutation; storage row r lies on the blk index r // 64. `candidates`: passage ids, repeats allowed. `lengths`: the live slots of a row are its first ones.
All inputs are finite; a program needn't handle non-finite values.
Results may differ from a plain program's by a relative error of at most 0.0003.
Values may be sent and summed in bfloat16 or wider, within the bound.
A program may use at most 64 MiB of HBM per device.

v0:
```python
import jax
import jax.numpy as jnp
from jax import lax
from jax.sharding import PartitionSpec as P

TOPN = 10


def score_table(rows_q, passages, lengths):
    queries_here = rows_q.shape[0]
    tokens = rows_q.shape[1]
    width = rows_q.shape[2]
    count = passages.shape[0]
    span = passages.shape[1]
    group = 4
    flat = rows_q.reshape(queries_here * tokens, width)
    blocks = passages.reshape(count // group, group * span, width)
    spans = lengths.reshape(count // group, group)

    def one_block(pair):
        piece, live_count = pair
        similar = lax.dot_general(
            flat, piece, (((1,), (1,)), ((), ())), preferred_element_type=jnp.float32
        )
        similar = similar.reshape(queries_here * tokens, group, span)
        live = lax.broadcasted_iota(jnp.int32, (group, span), 1) < live_count[:, None]
        best = jnp.max(jnp.where(live[None], similar, -1e30), axis=2)
        return jnp.sum(best.reshape(queries_here, tokens, group), axis=1) / tokens

    table = lax.map(one_block, (blocks, spans))
    return jnp.transpose(table, (1, 0, 2)).reshape(queries_here, count)


def shards(queries, passages, lengths, slot_of, candidates):
    table = score_table(lax.all_gather(queries, "blk", axis=0, tiled=True), passages, lengths)
    whole = lax.all_to_all(table, "blk", split_axis=0, concat_axis=1, tiled=True)
    score = jnp.take_along_axis(whole, jnp.take(slot_of, candidates, axis=0), axis=1)
    top = lax.top_k(score, TOPN)[0]
    return (score, top)


def solution(mesh):
    return jax.shard_map(
        shards,
        mesh=mesh,
        in_specs=(
            P(("parts", "blk", "sub", "rep"), None, None),
            P(("parts", "blk"), None, None),
            P(("parts", "blk")),
            P("parts"),
            P(("parts", "blk", "sub", "rep"), None),
        ),
        out_specs=(
            P(("parts", "blk", "sub", "rep"), None),
            P(("parts", "blk", "sub", "rep"), None),
        ),
        check_vma=False,
    )
```

profile of v0, /device:TPU:86, one launch (start us, length us, event | category | flops | bytes accessed | tf_op | source)
XLA Modules:
  0.0 134.1 jit_solution(3773919563160055687)
XLA Ops:
  0.7 0.7 reshape.67
  1.4 71.3 %all_gather.3 = bf16[64,32,128]{2,1,0:T(8,128)(2,1)S(1)} all-gather(bf16[4,32,128]{2,1,0:T(8,128)(2,1)} %param.7), channel_id=1, replica_groups=mesh['parts'=2,'blk'=16,'sub'=8,'rep'=2] {'blk'}, dimensions={0}, use_global_device_ids=true | all-gather | bytes 557056 | tf_op jit(solution)/shard_map/all_gather | solution.py:35
  72.6 31.7 %while.10 = (s32[]{:T(128)}, f32[16,64,4]{1,2,0:T(4,128)S(1)}, s32[16,4]{1,0:T(8,128)S(1)}, bf16[16,512,128]{2,1,0:T(8,128)(2,1)}, bf16[2048,128]{1,0:T(8,128)(2,1)S(1)}, /*index=5*/s32[]{:T(128)}, f32[]{:T(128)}) while((s32[]{:T(128)}, f32[16,64,4]{1,2,0:T(4,128)S(1)}, s32[16,4]{1,0:T(8,128)S(1)}, bf16[16,512,128]{2,1,0:T(8,128)(2,1)}, ...), condition=%wide.region_3.4_spmd, body=%wide.region_0.3_spmd.sunk | while | flops 270533120 | bytes 792725 | solution.py:30
  72.7 0.1 iota_compare_fusion.2
  72.7 1.7 %select_reduce_fusion.2 = f32[2048,4]{0,1:T(4,128)S(1)} fusion(pred[4,128]{1,0:T(4,128)(4,1)S(1)} %iota_compare_fusion.2, bf16[2048,128]{1,0:T(8,128)(2,1)S(1)} %get-tuple-element.93, bf16[16,512,128]{2,1,0:T(8,128)(2,1)} %get-tuple-element.92, s32[]{:T(128)S(6)} %copy.19), kind=kOutput, calls=%fused_computation.2.clone.1 | convolution fusion | flops 270524416 | bytes 688644 | tf_op jit(solution)/shard_map/while/body/eval_jaxpr/dot_general | solution.py:22
  74.4 0.1 reshape.95
  74.5 0.1 reduce_sum.10
  74.7 1.6 %select_reduce_fusion.2 = f32[2048,4]{0,1:T(4,128)S(1)} fusion(pred[4,128]{1,0:T(4,128)(4,1)S(1)} %iota_compare_fusion.2, bf16[2048,128]{1,0:T(8,128)(2,1)S(1)} %get-tuple-element.93, bf16[16,512,128]{2,1,0:T(8,128)(2,1)} %get-tuple-element.92, s32[]{:T(128)S(6)} %copy.19), kind=kOutput, calls=%fused_computation.2.clone.1 | convolution fusion | flops 270524416 | bytes 688644 | tf_op jit(solution)/shard_map/while/body/eval_jaxpr/dot_general | solution.py:22
  76.4 0.1 reshape.95
  76.5 0.1 reduce_sum.10
  76.7 1.6 %select_reduce_fusion.2 = f32[2048,4]{0,1:T(4,128)S(1)} fusion(pred[4,128]{1,0:T(4,128)(4,1)S(1)} %iota_compare_fusion.2, bf16[2048,128]{1,0:T(8,128)(2,1)S(1)} %get-tuple-element.93, bf16[16,512,128]{2,1,0:T(8,128)(2,1)} %get-tuple-element.92, s32[]{:T(128)S(6)} %copy.19), kind=kOutput, calls=%fused_computation.2.clone.1 | convolution fusion | flops 270524416 | bytes 688644 | tf_op jit(solution)/shard_map/while/body/eval_jaxpr/dot_general | solution.py:22
  78.3 0.1 reshape.95
  78.4 0.1 reduce_sum.10
  78.7 1.6 %select_reduce_fusion.2 = f32[2048,4]{0,1:T(4,128)S(1)} fusion(pred[4,128]{1,0:T(4,128)(4,1)S(1)} %iota_compare_fusion.2, bf16[2048,128]{1,0:T(8,128)(2,1)S(1)} %get-tuple-element.93, bf16[16,512,128]{2,1,0:T(8,128)(2,1)} %get-tuple-element.92, s32[]{:T(128)S(6)} %copy.19), kind=kOutput, calls=%fused_computation.2.clone.1 | convolution fusion | flops 270524416 | bytes 688644 | tf_op jit(solution)/shard_map/while/body/eval_jaxpr/dot_general | solution.py:22
  80.3 0.1 reshape.95
  80.4 0.1 reduce_sum.10
  80.7 1.6 %select_reduce_fusion.2 = f32[2048,4]{0,1:T(4,128)S(1)} fusion(pred[4,128]{1,0:T(4,128)(4,1)S(1)} %iota_compare_fusion.2, bf16[2048,128]{1,0:T(8,128)(2,1)S(1)} %get-tuple-element.93, bf16[16,512,128]{2,1,0:T(8,128)(2,1)} %get-tuple-element.92, s32[]{:T(128)S(6)} %copy.19), kind=kOutput, calls=%fused_computation.2.clone.1 | convolution fusion | flops 270524416 | bytes 688644 | tf_op jit(solution)/shard_map/while/body/eval_jaxpr/dot_general | solution.py:22
  82.3 0.1 reshape.95
  82.4 0.1 reduce_sum.10
  82.6 1.6 %select_reduce_fusion.2 = f32[2048,4]{0,1:T(4,128)S(1)} fusion(pred[4,128]{1,0:T(4,128)(4,1)S(1)} %iota_compare_fusion.2, bf16[2048,128]{1,0:T(8,128)(2,1)S(1)} %get-tuple-element.93, bf16[16,512,128]{2,1,0:T(8,128)(2,1)} %get-tuple-element.92, s32[]{:T(128)S(6)} %copy.19), kind=kOutput, calls=%fused_computation.2.clone.1 | convolution fusion | flops 270524416 | bytes 688644 | tf_op jit(solution)/shard_map/while/body/eval_jaxpr/dot_general | solution.py:22
  84.3 0.1 reshape.95
  84.4 0.1 reduce_sum.10
  84.6 1.6 %select_reduce_fusion.2 = f32[2048,4]{0,1:T(4,128)S(1)} fusion(pred[4,128]{1,0:T(4,128)(4,1)S(1)} %iota_compare_fusion.2, bf16[2048,128]{1,0:T(8,128)(2,1)S(1)} %get-tuple-element.93, bf16[16,512,128]{2,1,0:T(8,128)(2,1)} %get-tuple-element.92, s32[]{:T(128)S(6)} %copy.19), kind=kOutput, calls=%fused_computation.2.clone.1 | convolution fusion | flops 270524416 | bytes 688644 | tf_op jit(solution)/shard_map/while/body/eval_jaxpr/dot_general | solution.py:22
  86.3 0.1 reshape.95
  86.4 0.1 reduce_sum.10
  86.6 1.6 %select_reduce_fusion.2 = f32[2048,4]{0,1:T(4,128)S(1)} fusion(pred[4,128]{1,0:T(4,128)(4,1)S(1)} %iota_compare_fusion.2, bf16[2048,128]{1,0:T(8,128)(2,1)S(1)} %get-tuple-element.93, bf16[16,512,128]{2,1,0:T(8,128)(2,1)} %get-tuple-element.92, s32[]{:T(128)S(6)} %copy.19), kind=kOutput, calls=%fused_computation.2.clone.1 | convolution fusion | flops 270524416 | bytes 688644 | tf_op jit(solution)/shard_map/while/body/eval_jaxpr/dot_general | solution.py:22
  88.2 0.1 reshape.95
  88.3 0.1 reduce_sum.10
  88.6 1.6 %select_reduce_fusion.2 = f32[2048,4]{0,1:T(4,128)S(1)} fusion(pred[4,128]{1,0:T(4,128)(4,1)S(1)} %iota_compare_fusion.2, bf16[2048,128]{1,0:T(8,128)(2,1)S(1)} %get-tuple-element.93, bf16[16,512,128]{2,1,0:T(8,128)(2,1)} %get-tuple-element.92, s32[]{:T(128)S(6)} %copy.19), kind=kOutput, calls=%fused_computation.2.clone.1 | convolution fusion | flops 270524416 | bytes 688644 | tf_op jit(solution)/shard_map/while/body/eval_jaxpr/dot_general | solution.py:22
  90.2 0.1 reshape.95
  90.3 0.1 reduce_sum.10
  90.6 1.6 %select_reduce_fusion.2 = f32[2048,4]{0,1:T(4,128)S(1)} fusion(pred[4,128]{1,0:T(4,128)(4,1)S(1)} %iota_compare_fusion.2, bf16[2048,128]{1,0:T(8,128)(2,1)S(1)} %get-tuple-element.93, bf16[16,512,128]{2,1,0:T(8,128)(2,1)} %get-tuple-element.92, s32[]{:T(128)S(6)} %copy.19), kind=kOutput, calls=%fused_computation.2.clone.1 | convolution fusion | flops 270524416 | bytes 688644 | tf_op jit(solution)/shard_map/while/body/eval_jaxpr/dot_general | solution.py:22
  92.2 0.1 reshape.95
  92.3 0.1 reduce_sum.10
  92.5 1.6 %select_reduce_fusion.2 = f32[2048,4]{0,1:T(4,128)S(1)} fusion(pred[4,128]{1,0:T(4,128)(4,1)S(1)} %iota_compare_fusion.2, bf16[2048,128]{1,0:T(8,128)(2,1)S(1)} %get-tuple-element.93, bf16[16,512,128]{2,1,0:T(8,128)(2,1)} %get-tuple-element.92, s32[]{:T(128)S(6)} %copy.19), kind=kOutput, calls=%fused_computation.2.clone.1 | convolution fusion | flops 270524416 | bytes 688644 | tf_op jit(solution)/shard_map/while/body/eval_jaxpr/dot_general | solution.py:22
  94.2 0.1 reshape.95
  94.3 0.1 reduce_sum.10
  94.5 1.6 %select_reduce_fusion.2 = f32[2048,4]{0,1:T(4,128)S(1)} fusion(pred[4,128]{1,0:T(4,128)(4,1)S(1)} %iota_compare_fusion.2, bf16[2048,128]{1,0:T(8,128)(2,1)S(1)} %get-tuple-element.93, bf16[16,512,128]{2,1,0:T(8,128)(2,1)} %get-tuple-element.92, s32[]{:T(128)S(6)} %copy.19), kind=kOutput, calls=%fused_computation.2.clone.1 | convolution fusion | flops 270524416 | bytes 688644 | tf_op jit(solution)/shard_map/while/body/eval_jaxpr/dot_general | solution.py:22
  96.2 0.1 reshape.95
  96.3 0.1 reduce_sum.10
  96.5 1.6 %select_reduce_fusion.2 = f32[2048,4]{0,1:T(4,128)S(1)} fusion(pred[4,128]{1,0:T(4,128)(4,1)S(1)} %iota_compare_fusion.2, bf16[2048,128]{1,0:T(8,128)(2,1)S(1)} %get-tuple-element.93, bf16[16,512,128]{2,1,0:T(8,128)(2,1)} %get-tuple-element.92, s32[]{:T(128)S(6)} %copy.19), kind=kOutput, calls=%fused_computation.2.clone.1 | convolution fusion | flops 270524416 | bytes 688644 | tf_op jit(solution)/shard_map/while/body/eval_jaxpr/dot_general | solution.py:22
  98.1 0.1 reshape.95
  98.2 0.1 reduce_sum.10
  98.5 1.6 %select_reduce_fusion.2 = f32[2048,4]{0,1:T(4,128)S(1)} fusion(pred[4,128]{1,0:T(4,128)(4,1)S(1)} %iota_compare_fusion.2, bf16[2048,128]{1,0:T(8,128)(2,1)S(1)} %get-tuple-element.93, bf16[16,512,128]{2,1,0:T(8,128)(2,1)} %get-tuple-element.92, s32[]{:T(128)S(6)} %copy.19), kind=kOutput, calls=%fused_computation.2.clone.1 | convolution fusion | flops 270524416 | bytes 688644 | tf_op jit(solution)/shard_map/while/body/eval_jaxpr/dot_general | solution.py:22
  100.1 0.1 reshape.95
  100.2 0.1 reduce_sum.10
  100.5 1.6 %select_reduce_fusion.2 = f32[2048,4]{0,1:T(4,128)S(1)} fusion(pred[4,128]{1,0:T(4,128)(4,1)S(1)} %iota_compare_fusion.2, bf16[2048,128]{1,0:T(8,128)(2,1)S(1)} %get-tuple-element.93, bf16[16,512,128]{2,1,0:T(8,128)(2,1)} %get-tuple-element.92, s32[]{:T(128)S(6)} %copy.19), kind=kOutput, calls=%fused_computation.2.clone.1 | convolution fusion | flops 270524416 | bytes 688644 | tf_op jit(solution)/shard_map/while/body/eval_jaxpr/dot_general | solution.py:22
  102.1 0.1 reshape.95
  102.2 0.1 reduce_sum.10
  102.4 1.6 %select_reduce_fusion.2 = f32[2048,4]{0,1:T(4,128)S(1)} fusion(pred[4,128]{1,0:T(4,128)(4,1)S(1)} %iota_compare_fusion.2, bf16[2048,128]{1,0:T(8,128)(2,1)S(1)} %get-tuple-element.93, bf16[16,512,128]{2,1,0:T(8,128)(2,1)} %get-tuple-element.92, s32[]{:T(128)S(6)} %copy.19), kind=kOutput, calls=%fused_computation.2.clone.1 | convolution fusion | flops 270524416 | bytes 688644 | tf_op jit(solution)/shard_map/while/body/eval_jaxpr/dot_general | solution.py:22
  104.1 0.1 reshape.95
  104.2 0.1 reduce_sum.10
  104.3 0.3 reshape.91
  104.6 0.3 copy.13
  104.9 0.7 reshape.92
  105.6 3.9 %all-to-all-start = ((f32[16,1,256]{2,1,0:T(1,128)}), f32[16,1,256]{2,1,0:T(1,128)S(1)}, u32[]{:S(2)}, u32[]{:S(2)}) async-start(f32[16,1,256]{2,1,0:T(1,128)} %reshape.92), calls=%async_computation | async-start | bytes 32768 | tf_op jit(solution)/shard_map/all_to_all | solution.py:36
  109.6 4.5 %gather_fusion = s32[1024]{0:T(1024)S(1)} fusion(s32[1024]{0:T(1024)S(1)} %copy-done, s32[1024]{0:T(1024)S(1)} %broadcast_clamp_fusion), kind=kCustom, calls=%fused_computation | custom fusion | bytes 12288 | tf_op jit(solution)/shard_map/jit(_take)/gather | solution.py:37
  114.2 7.5 %all-to-all-done = f32[16,1,256]{2,1,0:T(1,128)S(1)} async-done(((f32[16,1,256]{2,1,0:T(1,128)}), f32[16,1,256]{2,1,0:T(1,128)S(1)}, u32[]{:S(2)}, u32[]{:S(2)}) %all-to-all-start) | async-done | bytes 16416 | tf_op jit(solution)/shard_map/all_to_all | solution.py:36
  121.6 0.5 broadcast.70
  122.2 0.7 reduce
  122.8 0.1 reshape.93
  122.9 0.1 all_to_all.17
  123.0 9.1 %gather_fusion.1 = f32[1024]{0:T(1024)S(1)} fusion(f32[4,1024]{1,0:T(4,128)S(1)} %all_to_all.17, s32[1024]{0:T(1024)S(1)} %bitcast.43), kind=kCustom, calls=%fused_computation.1 | custom fusion | bytes 16384 | tf_op jit(solution)/shard_map/jit(take_along_axis)/gather | solution.py:37
  132.2 1.9 %sort_prefixfusion = f32[4,10]{1,0:T(4,128)} fusion(f32[4,256]{1,0:T(4,128)S(1)} %and_select_fusion), kind=kCustom, calls=%top_k.9.sort_prefix | custom fusion | flops 10240 | bytes 4256 | tf_op jit(solution)/shard_map/top_k | solution.py:38
  (63 shorter events, 1.6 us)
Async XLA Ops:
  0.6 109.0 %copy-start = (s32[1024]{0:T(1024)S(1)}, s32[1024]{0:T(1024)}, u32[]{:S(2)}) copy-start(s32[1024]{0:T(1024)} %param.10) | copy-start | bytes 12292
  72.6 36.9 %copy-start.1 = (s32[4,256]{1,0:T(4,128)S(1)}, s32[4,256]{1,0:T(4,128)}, u32[]{:S(2)}) copy-start(s32[4,256]{1,0:T(4,128)} %param.11) | copy-start | bytes 12292
  105.6 16.0 %all-to-all-start = ((f32[16,1,256]{2,1,0:T(1,128)}), f32[16,1,256]{2,1,0:T(1,128)S(1)}, u32[]{:S(2)}, u32[]{:S(2)}) async-start(f32[16,1,256]{2,1,0:T(1,128)} %reshape.92), calls=%async_computation | async-start | bytes 32768 | tf_op jit(solution)/shard_map/all_to_all | solution.py:36
  132.2 1.9 %copy-start.2 = (f32[4,256]{1,0:T(4,128)}, f32[4,256]{1,0:T(4,128)S(1)}, u32[]{:S(2)}) copy-start(f32[4,256]{1,0:T(4,128)S(1)} %and_select_fusion) | copy-start | bytes 12292
where the time goes:
time: 135 us; the launch traced here: 134 us
  blocking collectives  71.3 us (53%)
  matrix products  26.2 us (19%)
  local copies, waits for them, and re-layouts  18.1 us (13%)
  waiting for transfers between devices  7.45 us (6%)
  other arithmetic  5.8 us (4%)
  starting transfers between devices  3.93 us (3%)
    all_gather x1, blocking collectives, shards(): lax.all_gather(queries, 'blk', axis=0, tiled=True)  71.3 us
    dot_general x16, matrix products, one_block(): lax.dot_general(flat, piece, (((1,), (1,)), ((), ())), preferred_element_...  26.2 us
    gather x2, local copies, waits for them, and re-layouts, shards(): jnp.take_along_axis(whole, jnp.take(slot_of, candidates, axis=0), axis=1)  9.13 us
    all_to_all x1, waiting for transfers between devices, shards(): lax.all_to_all(table, 'blk', split_axis=0, concat_axis=1, tiled=True)  7.45 us
    gather x2, local copies, waits for them, and re-layouts, shards(): jnp.take(slot_of, candidates, axis=0)  4.54 us
    all_to_all x1, starting transfers between devices, shards(): lax.all_to_all(table, 'blk', split_axis=0, concat_axis=1, tiled=True)  3.93 us
  transfers between devices with their start and end apart: 1, of which 1 were waited for; matrix products, arithmetic and copies ran while one was open for 3% of the time, Pallas kernels for 0%

commit v1 on v0

--- a/solution.py
+++ b/solution.py
@@ -4,6 +4,12 @@
 from jax.sharding import PartitionSpec as P
 
 TOPN = 10
+
+
+def trade_parts(x, axis, split, join):
+    pieces = jnp.split(x, lax.axis_size(axis), axis=split)
+    incoming = lax.all_to_all(jnp.stack(pieces), axis, 0, 0)
+    return jnp.concatenate(incoming, axis=join)
 
 
 def score_table(rows_q, passages, lengths):
@@ -33,7 +39,7 @@
 
 def shards(queries, passages, lengths, slot_of, candidates):
     table = score_table(lax.all_gather(queries, "blk", axis=0, tiled=True), passages, lengths)
-    whole = lax.all_to_all(table, "blk", split_axis=0, concat_axis=1, tiled=True)
+    whole = trade_parts(table, "blk", 0, 1)
     score = jnp.take_along_axis(whole, jnp.take(slot_of, candidates, axis=0), axis=1)
     top = lax.top_k(score, TOPN)[0]
     return (score, top)

time: 135 us -> 134 us (level)
  the two profiles are of different devices: /device:TPU:86 before, /device:TPU:92 now
where the time goes in v1:
time: 134 us
  blocking collectives  71.3 us (53%)
  matrix products  26.2 us (20%)
  local copies, waits for them, and re-layouts  17.5 us (13%)
  waiting for transfers between devices  7.45 us (6%)
  other arithmetic  5.8 us (4%)
  starting transfers between devices  3.93 us (3%)
    all_gather x1, blocking collectives, shards(): lax.all_gather(queries, 'blk', axis=0, tiled=True)  71.3 us
    dot_general x16, matrix products, one_block(): lax.dot_general(flat, piece, (((1,), (1,)), ((), ())), preferred_element_...  26.2 us
    all_to_all x1, waiting for transfers between devices, trade_parts(): incoming = lax.all_to_all(jnp.stack(pieces), axis, 0, 0)  7.45 us
    gather x2, local copies, waits for them, and re-layouts, shards(): jnp.take_along_axis(whole, jnp.take(slot_of, candidates, axis=0), axis=1)  7.3 us
    gather x2, local copies, waits for them, and re-layouts, shards(): jnp.take(slot_of, candidates, axis=0)  4.54 us
    all_to_all x1, starting transfers between devices, trade_parts(): incoming = lax.all_to_all(jnp.stack(pieces), axis, 0, 0)  3.93 us
  transfers between devices with their start and end apart: 1, of which 1 were waited for; matrix products, arithmetic and copies ran while one was open for 3% of the time, Pallas kernels for 0%

profile of v1, /device:TPU:92, one launch (start us, length us, event | category | flops | bytes accessed | tf_op | source)
XLA Modules:
  0.0 133.7 jit_solution(17445397237092499851)
XLA Ops:
  0.7 71.3 %all_gather.3 = bf16[64,32,128]{2,1,0:T(8,128)(2,1)S(1)} all-gather(bf16[4,32,128]{2,1,0:T(8,128)(2,1)} %param.7), channel_id=1, replica_groups=mesh['parts'=2,'blk'=16,'sub'=8,'rep'=2] {'blk'}, dimensions={0}, use_global_device_ids=true | all-gather | bytes 557056 | tf_op jit(solution)/shard_map/all_gather | solution.py:41
  71.9 0.7 reshape.101
  72.7 31.7 %while.10 = (s32[]{:T(128)}, f32[16,64,4]{1,2,0:T(4,128)S(1)}, s32[16,4]{1,0:T(8,128)S(1)}, bf16[16,512,128]{2,1,0:T(8,128)(2,1)}, bf16[2048,128]{1,0:T(8,128)(2,1)S(1)}, /*index=5*/s32[]{:T(128)}, f32[]{:T(128)}) while((s32[]{:T(128)}, f32[16,64,4]{1,2,0:T(4,128)S(1)}, s32[16,4]{1,0:T(8,128)S(1)}, bf16[16,512,128]{2,1,0:T(8,128)(2,1)}, ...), condition=%wide.region_3.4_spmd, body=%wide.region_0.3_spmd.sunk | while | flops 270533120 | bytes 793225 | solution.py:36
  72.7 0.1 iota_compare_fusion.2
  72.8 1.6 %select_reduce_fusion.2 = f32[2048,4]{0,1:T(4,128)S(1)} fusion(pred[4,128]{1,0:T(4,128)(4,1)S(1)} %iota_compare_fusion.2, bf16[2048,128]{1,0:T(8,128)(2,1)S(1)} %get-tuple-element.109, bf16[16,512,128]{2,1,0:T(8,128)(2,1)} %get-tuple-element.108, s32[]{:T(128)} %get-tuple-element.98), kind=kOutput, calls=%fused_computation.2.clone.1 | convolution fusion | flops 270524416 | bytes 689152 | tf_op jit(solution)/shard_map/while/body/eval_jaxpr/dot_general | solution.py:28
  74.4 0.1 reshape.130
  74.5 0.1 reduce_sum.10
  74.7 0.1 iota_compare_fusion.2
  74.8 1.6 %select_reduce_fusion.2 = f32[2048,4]{0,1:T(4,128)S(1)} fusion(pred[4,128]{1,0:T(4,128)(4,1)S(1)} %iota_compare_fusion.2, bf16[2048,128]{1,0:T(8,128)(2,1)S(1)} %get-tuple-element.109, bf16[16,512,128]{2,1,0:T(8,128)(2,1)} %get-tuple-element.108, s32[]{:T(128)} %get-tuple-element.98), kind=kOutput, calls=%fused_computation.2.clone.1 | convolution fusion | flops 270524416 | bytes 689152 | tf_op jit(solution)/shard_map/while/body/eval_jaxpr/dot_general | solution.py:28
  76.4 0.1 reshape.130
  76.5 0.1 reduce_sum.10
  76.8 1.6 %select_reduce_fusion.2 = f32[2048,4]{0,1:T(4,128)S(1)} fusion(pred[4,128]{1,0:T(4,128)(4,1)S(1)} %iota_compare_fusion.2, bf16[2048,128]{1,0:T(8,128)(2,1)S(1)} %get-tuple-element.109, bf16[16,512,128]{2,1,0:T(8,128)(2,1)} %get-tuple-element.108, s32[]{:T(128)} %get-tuple-element.98), kind=kOutput, calls=%fused_computation.2.clone.1 | convolution fusion | flops 270524416 | bytes 689152 | tf_op jit(solution)/shard_map/while/body/eval_jaxpr/dot_general | solution.py:28
  78.4 0.1 reshape.130
  78.5 0.1 reduce_sum.10
  78.7 1.6 %select_reduce_fusion.2 = f32[2048,4]{0,1:T(4,128)S(1)} fusion(pred[4,128]{1,0:T(4,128)(4,1)S(1)} %iota_compare_fusion.2, bf16[2048,128]{1,0:T(8,128)(2,1)S(1)} %get-tuple-element.109, bf16[16,512,128]{2,1,0:T(8,128)(2,1)} %get-tuple-element.108, s32[]{:T(128)} %get-tuple-element.98), kind=kOutput, calls=%fused_computation.2.clone.1 | convolution fusion | flops 270524416 | bytes 689152 | tf_op jit(solution)/shard_map/while/body/eval_jaxpr/dot_general | solution.py:28
  80.4 0.1 reshape.130
  80.5 0.1 reduce_sum.10
  80.7 1.6 %select_reduce_fusion.2 = f32[2048,4]{0,1:T(4,128)S(1)} fusion(pred[4,128]{1,0:T(4,128)(4,1)S(1)} %iota_compare_fusion.2, bf16[2048,128]{1,0:T(8,128)(2,1)S(1)} %get-tuple-element.109, bf16[16,512,128]{2,1,0:T(8,128)(2,1)} %get-tuple-element.108, s32[]{:T(128)} %get-tuple-element.98), kind=kOutput, calls=%fused_computation.2.clone.1 | convolution fusion | flops 270524416 | bytes 689152 | tf_op jit(solution)/shard_map/while/body/eval_jaxpr/dot_general | solution.py:28
  82.4 0.1 reshape.130
  82.5 0.1 reduce_sum.10
  82.7 1.6 %select_reduce_fusion.2 = f32[2048,4]{0,1:T(4,128)S(1)} fusion(pred[4,128]{1,0:T(4,128)(4,1)S(1)} %iota_compare_fusion.2, bf16[2048,128]{1,0:T(8,128)(2,1)S(1)} %get-tuple-element.109, bf16[16,512,128]{2,1,0:T(8,128)(2,1)} %get-tuple-element.108, s32[]{:T(128)} %get-tuple-element.98), kind=kOutput, calls=%fused_computation.2.clone.1 | convolution fusion | flops 270524416 | bytes 689152 | tf_op jit(solution)/shard_map/while/body/eval_jaxpr/dot_general | solution.py:28
  84.3 0.1 reshape.130
  84.4 0.1 reduce_sum.10
  84.7 1.6 %select_reduce_fusion.2 = f32[2048,4]{0,1:T(4,128)S(1)} fusion(pred[4,128]{1,0:T(4,128)(4,1)S(1)} %iota_compare_fusion.2, bf16[2048,128]{1,0:T(8,128)(2,1)S(1)} %get-tuple-element.109, bf16[16,512,128]{2,1,0:T(8,128)(2,1)} %get-tuple-element.108, s32[]{:T(128)} %get-tuple-element.98), kind=kOutput, calls=%fused_computation.2.clone.1 | convolution fusion | flops 270524416 | bytes 689152 | tf_op jit(solution)/shard_map/while/body/eval_jaxpr/dot_general | solution.py:28
  86.3 0.1 reshape.130
  86.4 0.1 reduce_sum.10
  86.7 1.6 %select_reduce_fusion.2 = f32[2048,4]{0,1:T(4,128)S(1)} fusion(pred[4,128]{1,0:T(4,128)(4,1)S(1)} %iota_compare_fusion.2, bf16[2048,128]{1,0:T(8,128)(2,1)S(1)} %get-tuple-element.109, bf16[16,512,128]{2,1,0:T(8,128)(2,1)} %get-tuple-element.108, s32[]{:T(128)} %get-tuple-element.98), kind=kOutput, calls=%fused_computation.2.clone.1 | convolution fusion | flops 270524416 | bytes 689152 | tf_op jit(solution)/shard_map/while/body/eval_jaxpr/dot_general | solution.py:28
  88.3 0.1 reshape.130
  88.4 0.1 reduce_sum.10
  88.6 1.6 %select_reduce_fusion.2 = f32[2048,4]{0,1:T(4,128)S(1)} fusion(pred[4,128]{1,0:T(4,128)(4,1)S(1)} %iota_compare_fusion.2, bf16[2048,128]{1,0:T(8,128)(2,1)S(1)} %get-tuple-element.109, bf16[16,512,128]{2,1,0:T(8,128)(2,1)} %get-tuple-element.108, s32[]{:T(128)} %get-tuple-element.98), kind=kOutput, calls=%fused_computation.2.clone.1 | convolution fusion | flops 270524416 | bytes 689152 | tf_op jit(solution)/shard_map/while/body/eval_jaxpr/dot_general | solution.py:28
  90.3 0.1 reshape.130
  90.4 0.1 reduce_sum.10
  90.6 1.6 %select_reduce_fusion.2 = f32[2048,4]{0,1:T(4,128)S(1)} fusion(pred[4,128]{1,0:T(4,128)(4,1)S(1)} %iota_compare_fusion.2, bf16[2048,128]{1,0:T(8,128)(2,1)S(1)} %get-tuple-element.109, bf16[16,512,128]{2,1,0:T(8,128)(2,1)} %get-tuple-element.108, s32[]{:T(128)} %get-tuple-element.98), kind=kOutput, calls=%fused_computation.2.clone.1 | convolution fusion | flops 270524416 | bytes 689152 | tf_op jit(solution)/shard_map/while/body/eval_jaxpr/dot_general | solution.py:28
  92.3 0.1 reshape.130
  92.4 0.1 reduce_sum.10
  92.6 1.6 %select_reduce_fusion.2 = f32[2048,4]{0,1:T(4,128)S(1)} fusion(pred[4,128]{1,0:T(4,128)(4,1)S(1)} %iota_compare_fusion.2, bf16[2048,128]{1,0:T(8,128)(2,1)S(1)} %get-tuple-element.109, bf16[16,512,128]{2,1,0:T(8,128)(2,1)} %get-tuple-element.108, s32[]{:T(128)} %get-tuple-element.98), kind=kOutput, calls=%fused_computation.2.clone.1 | convolution fusion | flops 270524416 | bytes 689152 | tf_op jit(solution)/shard_map/while/body/eval_jaxpr/dot_general | solution.py:28
  94.2 0.1 reshape.130
  94.3 0.1 reduce_sum.10
  94.6 1.6 %select_reduce_fusion.2 = f32[2048,4]{0,1:T(4,128)S(1)} fusion(pred[4,128]{1,0:T(4,128)(4,1)S(1)} %iota_compare_fusion.2, bf16[2048,128]{1,0:T(8,128)(2,1)S(1)} %get-tuple-element.109, bf16[16,512,128]{2,1,0:T(8,128)(2,1)} %get-tuple-element.108, s32[]{:T(128)} %get-tuple-element.98), kind=kOutput, calls=%fused_computation.2.clone.1 | convolution fusion | flops 270524416 | bytes 689152 | tf_op jit(solution)/shard_map/while/body/eval_jaxpr/dot_general | solution.py:28
  96.2 0.1 reshape.130
  96.3 0.1 reduce_sum.10
  96.5 1.6 %select_reduce_fusion.2 = f32[2048,4]{0,1:T(4,128)S(1)} fusion(pred[4,128]{1,0:T(4,128)(4,1)S(1)} %iota_compare_fusion.2, bf16[2048,128]{1,0:T(8,128)(2,1)S(1)} %get-tuple-element.109, bf16[16,512,128]{2,1,0:T(8,128)(2,1)} %get-tuple-element.108, s32[]{:T(128)} %get-tuple-element.98), kind=kOutput, calls=%fused_computation.2.clone.1 | convolution fusion | flops 270524416 | bytes 689152 | tf_op jit(solution)/shard_map/while/body/eval_jaxpr/dot_general | solution.py:28
  98.2 0.1 reshape.130
  98.3 0.1 reduce_sum.10
  98.5 1.6 %select_reduce_fusion.2 = f32[2048,4]{0,1:T(4,128)S(1)} fusion(pred[4,128]{1,0:T(4,128)(4,1)S(1)} %iota_compare_fusion.2, bf16[2048,128]{1,0:T(8,128)(2,1)S(1)} %get-tuple-element.109, bf16[16,512,128]{2,1,0:T(8,128)(2,1)} %get-tuple-element.108, s32[]{:T(128)} %get-tuple-element.98), kind=kOutput, calls=%fused_computation.2.clone.1 | convolution fusion | flops 270524416 | bytes 689152 | tf_op jit(solution)/shard_map/while/body/eval_jaxpr/dot_general | solution.py:28
  100.2 0.1 reshape.130
  100.3 0.1 reduce_sum.10
  100.5 1.6 %select_reduce_fusion.2 = f32[2048,4]{0,1:T(4,128)S(1)} fusion(pred[4,128]{1,0:T(4,128)(4,1)S(1)} %iota_compare_fusion.2, bf16[2048,128]{1,0:T(8,128)(2,1)S(1)} %get-tuple-element.109, bf16[16,512,128]{2,1,0:T(8,128)(2,1)} %get-tuple-element.108, s32[]{:T(128)} %get-tuple-element.98), kind=kOutput, calls=%fused_computation.2.clone.1 | convolution fusion | flops 270524416 | bytes 689152 | tf_op jit(solution)/shard_map/while/body/eval_jaxpr/dot_general | solution.py:28
  102.2 0.1 reshape.130
  102.2 0.1 reduce_sum.10
  102.5 1.6 %select_reduce_fusion.2 = f32[2048,4]{0,1:T(4,128)S(1)} fusion(pred[4,128]{1,0:T(4,128)(4,1)S(1)} %iota_compare_fusion.2, bf16[2048,128]{1,0:T(8,128)(2,1)S(1)} %get-tuple-element.109, bf16[16,512,128]{2,1,0:T(8,128)(2,1)} %get-tuple-element.108, s32[]{:T(128)} %get-tuple-element.98), kind=kOutput, calls=%fused_computation.2.clone.1 | convolution fusion | flops 270524416 | bytes 689152 | tf_op jit(solution)/shard_map/while/body/eval_jaxpr/dot_general | solution.py:28
  104.1 0.1 reshape.130
  104.2 0.1 reduce_sum.10
  104.4 0.3 fusion.7
  106.2 0.7 reshape.127
  106.8 3.9 %all-to-all-start = ((f32[16,1,256]{2,1,0:T(1,128)}), f32[16,1,256]{2,1,0:T(1,128)S(1)}, u32[]{:S(2)}, u32[]{:S(2)}) async-start(f32[16,1,256]{2,1,0:T(1,128)} %reshape.127), calls=%async_computation | async-start | bytes 32768 | tf_op jit(solution)/shard_map/all_to_all | solution.py:11
  110.8 4.5 %gather_fusion = s32[1024]{0:T(1024)S(1)} fusion(s32[1024]{0:T(1024)S(1)} %copy-done, s32[1024]{0:T(1024)S(1)} %broadcast_clamp_fusion), kind=kCustom, calls=%fused_computation | custom fusion | bytes 12288 | tf_op jit(solution)/shard_map/jit(_take)/gather | solution.py:43
  115.4 7.5 %all-to-all-done = f32[16,1,256]{2,1,0:T(1,128)S(1)} async-done(((f32[16,1,256]{2,1,0:T(1,128)}), f32[16,1,256]{2,1,0:T(1,128)S(1)}, u32[]{:S(2)}, u32[]{:S(2)}) %all-to-all-start) | async-done | bytes 16416 | tf_op jit(solution)/shard_map/all_to_all | solution.py:11
  122.9 0.5 broadcast.70
  123.4 0.7 reduce
  124.1 0.1 reshape.128
  124.2 0.2 copy.75
  124.4 7.3 %gather_fusion.1 = f32[1024]{0:T(1024)S(1)} fusion(f32[4,1024]{0,1:T(8,128)S(1)} %bitcast.59, s32[1024]{0:T(1024)S(1)} %bitcast.58), kind=kCustom, calls=%fused_computation.1 | custom fusion | bytes 16384 | tf_op jit(solution)/shard_map/jit(take_along_axis)/gather | solution.py:43
  131.8 1.9 %sort_prefixfusion = f32[4,10]{1,0:T(4,128)} fusion(f32[4,256]{1,0:T(4,128)S(1)} %and_select_fusion), kind=kCustom, calls=%top_k.9.sort_prefix | custom fusion | flops 10240 | bytes 4256 | tf_op jit(solution)/shard_map/top_k | solution.py:44
  (93 shorter events, 2.8 us)
Async XLA Ops:
  0.6 110.2 %copy-start = (s32[1024]{0:T(1024)S(1)}, s32[1024]{0:T(1024)}, u32[]{:S(2)}) copy-start(s32[1024]{0:T(1024)} %param.10) | copy-start | bytes 12292
  72.7 38.1 %copy-start.1 = (s32[4,256]{1,0:T(4,128)S(1)}, s32[4,256]{1,0:T(4,128)}, u32[]{:S(2)}) copy-start(s32[4,256]{1,0:T(4,128)} %param.11) | copy-start | bytes 12292
  106.8 16.0 %all-to-all-start = ((f32[16,1,256]{2,1,0:T(1,128)}), f32[16,1,256]{2,1,0:T(1,128)S(1)}, u32[]{:S(2)}, u32[]{:S(2)}) async-start(f32[16,1,256]{2,1,0:T(1,128)} %reshape.127), calls=%async_computation | async-start | bytes 32768 | tf_op jit(solution)/shard_map/all_to_all | solution.py:11
  131.7 1.9 %copy-start.2 = (f32[4,256]{1,0:T(4,128)}, f32[4,256]{1,0:T(4,128)S(1)}, u32[]{:S(2)}) copy-start(f32[4,256]{1,0:T(4,128)S(1)} %and_select_fusion) | copy-start | bytes 12292
